TPU v7x, 32 devices: a whole 2x2x4 slice. The times are simulated.
32 devices in a mesh: seq: 8 (over z, y), grp: 4 (over x, core).
Axes of the slice: x: 2, y: 2, z: 4, core: 2. Of those that a mesh axis runs over, the one named last changes fastest.
Arguments:
- hidden: bfloat16 [256, 8192], P('grp', 'seq'), may hold values from -6 to 6
- w_qkv: bfloat16 [8192, 10240], P('seq', 'grp'), may hold values from -0.0625 to 0.0625
- b_qkv: float32 [10240], P('grp'), may hold values from -3 to 3
- w_out: bfloat16 [8192, 8192], P('seq', 'grp'), may hold values from -0.0625 to 0.0625
- k_cache: bfloat16 [4, 32768, 1024], P('grp', 'seq'), may hold values from -600 to 600
- v_cache: bfloat16 [4, 32768, 1024], P('grp', 'seq'), may hold values from -6 to 6
- lengths: int32 [256], replicated, may hold values from 1 to 16384, as said below
- page_table: int32 [256, 128], replicated, may hold values from -1 to 255, as said below
- positions: int32 [3, 256], replicated, may hold values from 0 to 4095
- group_of: int32 [256], replicated, may hold values from 0 to 3, as said below
Outputs:
- mixed: bfloat16 [256, 8192], P('seq', 'grp')
Inputs may be any that keep to these rules, and one draw needn't show every extreme that they name: `group_of`: each group serves exactly 64 requests. `lengths`: each group has a request of exactly 16384 cached positions. `page_table`: entry j of row r is the page of request r's group pool (page p lies on that group's device p // 32 of seq) that holds its positions j * 128 to (j + 1) * 128 - 1, for j < ceil(lengths[r] / 128); later entries are -1; no page belongs to two requests.
All inputs are finite; a program needn't handle non-finite values.
Results may differ from a plain program's by a relative error of at most 0.015.
The roundings to bfloat16 on the way count: a program that leaves them out, or rounds other values in their place, can miss the bound.
Values may be sent and summed in bfloat16 or wider, within the bound.
A program may use at most 128 MiB of HBM per device.

v0:
```python
import math
import jax
import jax.numpy as jnp
from jax import lax
from jax.sharding import PartitionSpec as P

HQ = 64
KVH = 8
HD = 128
PAGE = 128
rope_base = 1000000.0
neg_fill = -1e30


def rotate_heads(values, places, col_start, head_dim, turned):
    row_count, col_count = values.shape
    columns = col_start + jnp.arange(col_count, dtype=jnp.int32)
    within = columns % head_dim
    freq_index = within % (head_dim // 2)
    inverse_freq = jnp.exp(freq_index.astype(jnp.float32) * (-2.0 * math.log(rope_base) / head_dim))
    section = jnp.where(
        freq_index < head_dim // 8,
        0,
        jnp.where(freq_index < head_dim // 8 + 3 * head_dim // 16, 1, 2),
    )
    place_float = places.astype(jnp.float32)
    chosen = jnp.where(
        section[None, :] == 0,
        place_float[0][:, None],
        jnp.where(section[None, :] == 1, place_float[1][:, None], place_float[2][:, None]),
    )
    angles = chosen * inverse_freq[None, :]
    halves = values.reshape(row_count, col_count // head_dim, 2, head_dim // 2)
    partner = jnp.concatenate([-halves[:, :, 1:], halves[:, :, :1]], axis=2).reshape(
        row_count, col_count
    )
    rotated = values * jnp.cos(angles) + partner * jnp.sin(angles)
    return jnp.where((columns < turned)[None, :], rotated, values)


def shards(hidden, w_qkv, b_qkv, w_out, k_cache, v_cache, lengths, page_table, positions, group_of):
    seq_count = lax.axis_size("seq")
    grp_count = lax.axis_size("grp")
    seq_index = lax.axis_index("seq")
    grp_index = lax.axis_index("grp")
    request_total = group_of.shape[0]
    group_size = request_total // grp_count
    col_count = w_qkv.shape[1]
    col_start = grp_index * col_count
    turned = (HQ + KVH) * HD
    group_q = HQ // KVH
    score_scale = HD ** (-0.5)
    partial_sum = jnp.dot(
        lax.all_gather(hidden, "grp", axis=0, tiled=True), w_qkv, preferred_element_type=jnp.float32
    )
    request_ids = jnp.arange(request_total, dtype=jnp.int32)
    before = (group_of[None, :] < group_of[:, None]) | (group_of[None, :] == group_of[:, None]) & (
        request_ids[None, :] < request_ids[:, None]
    )
    restore = jnp.sum(before.astype(jnp.int32), axis=1)
    placed_at = restore[None, :] == request_ids[:, None]
    served_order = jnp.sum(jnp.where(placed_at, request_ids[None, :], 0), axis=1)
    served_ids = lax.dynamic_slice_in_dim(served_order, grp_index * group_size, group_size, 0)
    summed = lax.psum(partial_sum, "seq")
    fresh_rows = rotate_heads(summed + b_qkv[None, :], positions, col_start, HD, turned).astype(
        jnp.bfloat16
    )
    outgoing = fresh_rows[served_order].reshape(grp_count, group_size, col_count)
    incoming = lax.all_to_all(outgoing, "grp", split_axis=0, concat_axis=2, tiled=True)
    served_rows = incoming.reshape(group_size, grp_count * col_count)
    query_rows = served_rows[:, : HQ * HD]
    key_new = served_rows[:, HQ * HD : turned]
    value_new = served_rows[:, turned:]
    served_len = lengths[served_ids]
    served_table = page_table[served_ids]
    most_pages = page_table.shape[1]
    page_counts = (served_len + PAGE - 1) // PAGE
    logical = jnp.arange(most_pages, dtype=jnp.int32)
    pool_pages = k_cache.shape[1] // PAGE
    local_page = served_table - seq_index * pool_pages
    usable = (
        (logical[None, :] < page_counts[:, None]) & (local_page >= 0) & (local_page < pool_pages)
    )
    pool_ids = jnp.arange(pool_pages, dtype=jnp.int32)
    matched = usable[:, :, None] & (local_page[:, :, None] == pool_ids[None, None, :])
    owner_ids = jnp.arange(group_size, dtype=jnp.int32)
    page_owner = jnp.max(jnp.where(matched, owner_ids[:, None, None], -1), axis=(0, 1))
    page_number = jnp.max(jnp.where(matched, logical[None, :, None], 0), axis=(0, 1))
    present = page_owner >= 0
    holder = jnp.maximum(page_owner, 0)
    page_query = query_rows[holder].reshape(pool_pages, KVH, group_q, HD)
    page_keys = k_cache[0].reshape(pool_pages, PAGE, KVH, HD)
    page_values = v_cache[0].reshape(pool_pages, PAGE, KVH, HD)
    scores = (
        jnp.einsum("pkgd,ptkd->pkgt", page_query, page_keys, preferred_element_type=jnp.float32)
        * score_scale
    )
    places_in = page_number[:, None] * PAGE + jnp.arange(PAGE, dtype=jnp.int32)[None, :]
    alive_rows = present[:, None] & (places_in < served_len[holder][:, None])
    alive_wide = alive_rows[:, None, None, :]
    page_max = jnp.max(jnp.where(alive_wide, scores, neg_fill), axis=3)
    weights = jnp.exp(jnp.where(alive_wide, scores - page_max[..., None], neg_fill))
    page_total = jnp.sum(weights, axis=3).reshape(pool_pages, HQ)
    page_out = jnp.einsum(
        "pkgt,ptkd->pkgd",
        weights.astype(jnp.bfloat16),
        page_values,
        preferred_element_type=jnp.float32,
    ).reshape(pool_pages, HQ, HD)
    page_max = page_max.reshape(pool_pages, HQ)
    member = page_owner[:, None] == owner_ids[None, :]
    local_max = jnp.max(jnp.where(member[:, :, None], page_max[:, None, :], neg_fill), axis=0)
    factor = jnp.where(present[:, None], jnp.exp(page_max - local_max[holder]), 0.0)
    member_float = member.astype(jnp.float32)
    local_total = jnp.einsum(
        "pr,ph->rh", member_float, page_total * factor, precision=lax.Precision.HIGHEST
    )
    local_out = jnp.einsum(
        "pr,pe->re",
        member_float,
        (page_out * factor[..., None]).reshape(pool_pages, HQ * HD),
        precision=lax.Precision.HIGHEST,
    )
    new_score = (
        jnp.einsum(
            "rkgd,rkd->rkg",
            query_rows.reshape(group_size, KVH, group_q, HD),
            key_new.reshape(group_size, KVH, HD),
            preferred_element_type=jnp.float32,
        ).reshape(group_size, HQ)
        * score_scale
    )
    head_share = HQ // seq_count
    head_start = seq_index * head_share
    value_heads = jnp.broadcast_to(
        value_new.reshape(group_size, KVH, 1, HD), (group_size, KVH, group_q, HD)
    ).reshape(group_size, HQ, HD)
    value_here = lax.dynamic_slice_in_dim(value_heads, head_start, head_share, 1).astype(
        jnp.float32
    )
    new_here = lax.dynamic_slice_in_dim(new_score, head_start, head_share, 1)
    peak_score = lax.pmax(jnp.maximum(local_max, new_score), "seq")
    kept_scale = jnp.exp(local_max - peak_score)
    scaled_out = (local_out.reshape(group_size, HQ, HD) * kept_scale[..., None]).reshape(
        group_size, HQ * HD
    )
    shared_out, shared_total = (
        lax.psum_scatter(scaled_out, "seq", scatter_dimension=1, tiled=True),
        lax.psum_scatter(local_total * kept_scale, "seq", scatter_dimension=1, tiled=True),
    )
    peak_here = lax.dynamic_slice_in_dim(peak_score, head_start, head_share, 1)
    fresh_weight = jnp.exp(new_here - peak_here)
    denominator = shared_total + fresh_weight
    numerator = (
        shared_out.reshape(group_size, head_share, HD) + fresh_weight[..., None] * value_here
    )
    attended = (
        (numerator / denominator[..., None])
        .reshape(group_size, head_share * HD)
        .astype(jnp.bfloat16)
    )
    gathered = lax.all_gather(attended, "grp", axis=0, tiled=True)
    by_request = gathered[restore]
    return lax.psum_scatter(
        jnp.dot(by_request, w_out, preferred_element_type=jnp.float32).astype(jnp.bfloat16),
        "seq",
        scatter_dimension=0,
        tiled=True,
    )


def solution(mesh):
    placed = (
        P("grp", "seq"),
        P("seq", "grp"),
        P("grp"),
        P("seq", "grp"),
        P("grp", "seq", None),
        P("grp", "seq", None),
        P(),
        P(),
        P(),
        P(),
    )
    return jax.shard_map(
        shards, mesh=mesh, in_specs=placed, out_specs=P("seq", "grp"), check_vma=False
    )
```

profile of v0, /device:TPU:0, one launch (start us, length us, event | category | flops | bytes accessed | tf_op | source)
XLA Modules:
  0.0 401.6 jit_solution(12910051012480212838)
XLA Ops:
  6.5 9.0 %all_gather.6 = bf16[256,1024]{1,0:T(8,128)(2,1)S(1)} all-gather(bf16[64,1024]{1,0:T(8,128)(2,1)} %param.10), channel_id=1, replica_groups=mesh['seq'=8,'grp'=4] {'grp'}, dimensions={0}, use_global_device_ids=true | all-gather | bytes 655360 | tf_op jit(solution)/shard_map/all_gather | solution.py:54
  15.5 5.5 %fusion.40 = f32[256,2560]{1,0:T(8,128)} fusion(bf16[256,1024]{1,0:T(8,128)(2,1)S(1)} %all_gather.6, bf16[1024,2560]{1,0:T(8,128)(2,1)} %param.11), kind=kOutput, calls=%fused_computation.102 | convolution fusion | flops 1342177280 | bytes 8388608 | tf_op jit(solution)/shard_map/dot_general | solution.py:53
  24.9 113.1 %all-reduce.3.cloned.1.call-done = f32[256,2560]{1,0:T(8,128)} async-done(((f32[256,2560]{1,0:T(8,128)}), f32[256,2560]{1,0:T(8,128)}) %all-reduce.3.cloned.1.call-update) | async-done | bytes 2621456 | tf_op jit(solution)/shard_map/psum | solution.py:64
  138.0 3.6 broadcast_add_fusion
  141.6 2.1 copy.46
  144.1 2.1 copy.47
  146.2 11.8 %select_convert_fusion = bf16[256,2560]{1,0:T(8,128)(2,1)S(1)} fusion(f32[256,2560]{1,0:T(8,128)} %copy.47, f32[2560]{0:T(1024)S(1)} %multiply_exponential_fusion, f32[256]{0:T(256)S(1)} %bitcast.123, f32[256]{0:T(256)S(1)} %bitcast.124, f32[256]{0:T(256)S(1)} %bitcast.122, pred[2560]{0:T(1024)(128)(4,1)S(1)} %get-tuple-element.26, ...), kind=kLoop, calls=%fused_computation.12 | loop fusion | flops 5898240 | bytes 6584832 | tf_op jit(solution)/shard_map/convert_element_type | solution.py:65
  158.0 2.5 gather_fusion.3
  160.5 3.5 all-to-all-start
  165.1 8.8 %copy.68 = bf16[512,8,8,128]{3,2,1,0:T(8,128)(2,1)} copy(bf16[512,8,8,128]{3,1,2,0:T(8,128)(2,1)} %bitcast.100) | data formatting | bytes 16777216
  173.8 8.8 %copy.69 = bf16[512,8,8,128]{3,2,1,0:T(8,128)(2,1)} copy(bf16[512,8,8,128]{3,1,2,0:T(8,128)(2,1)} %bitcast.101) | data formatting | bytes 16777216
  184.9 1.7 gather_fusion.4
  187.8 6.9 %select_reduce_fusion.1 = (f32[32,8,8]{2,1,0:T(8,128)S(1)}, f32[32,8,8,128]{3,2,1,0:T(8,128)S(1)}) fusion(pred[32,128]{1,0:T(8,128)(4,1)S(1)} %fusion.25, bf16[32,8,8,128]{3,2,1,0:T(8,128)(2,1)S(1)} %bitcast.109, bf16[32,128,8,128]{3,2,1,0:T(8,128)(2,1)} %bitcast.97), kind=kOutput, calls=%fused_computation.26 | convolution fusion | flops 67893248 | bytes 9973760 | tf_op jit(solution)/shard_map/pkgd,ptkd->pkgt/dot_general | solution.py:95
  196.3 1.6 select_reduce_fusion
  197.9 2.0 gather_fusion.5
  205.6 35.0 %pmax.7 = f32[64,64]{0,1:T(8,128)S(1)} all-reduce(f32[64,64]{0,1:T(8,128)S(1)} %fusion.38), channel_id=1, replica_groups=mesh['seq'=8,'grp'=4] {'seq'}, use_global_device_ids=true, to_apply=%region_7.8 | all-reduce | flops 4096 | bytes 32768 | tf_op jit(solution)/shard_map/pmax | solution.py:142
  240.7 6.1 %fusion = f32[32,8,8,128]{3,2,1,0:T(8,128)S(1)} fusion(bf16[32,128,8,128]{3,2,1,0:T(8,128)(2,1)} %bitcast.96, f32[32,8,8,128]{3,2,1,0:T(8,128)S(1)} %get-tuple-element.21, f32[32,8,8]{2,1,0:T(8,128)S(1)} %get-tuple-element.20, pred[32,128]{1,0:T(8,128)(4,1)S(1)} %copy-done.6), kind=kOutput, calls=%fused_computation.7 | convolution fusion | flops 67895296 | bytes 10498048 | tf_op jit(solution)/shard_map/pkgt,ptkd->pkgd/dot_general | solution.py:104
  247.1 2.5 multiply_bitcast_fusion
  249.6 1.5 copy.96
  253.6 33.8 %all-reduce = f32[64,64]{0,1:T(8,128)S(1)} all-reduce(f32[64,64]{0,1:T(8,128)S(1)} %convolution_multiply_fusion), channel_id=3, replica_groups=mesh['seq'=8,'grp'=4] {'seq'}, use_global_device_ids=true, to_apply=%region_10.11.clone | all-reduce | flops 4096 | bytes 32768
  288.0 29.7 %reduce-scatter.3.cloned.1.call-done = f32[64,1024]{1,0:T(8,128)} async-done(((f32[64,8192]{1,0:T(8,128)}), f32[64,1024]{1,0:T(8,128)}) %reduce-scatter.3.cloned.1.call-update) | async-done | bytes 262160 | tf_op jit(solution)/shard_map/reduce_scatter | solution.py:148
  318.9 7.2 %all_gather.7 = bf16[256,1024]{1,0:T(8,128)(2,1)S(1)} all-gather(bf16[64,1024]{1,0:T(8,128)(2,1)S(1)} %bitcast.113), channel_id=1, replica_groups=mesh['seq'=8,'grp'=4] {'grp'}, dimensions={0}, use_global_device_ids=true | all-gather | bytes 655360 | tf_op jit(solution)/shard_map/all_gather | solution.py:162
  327.3 4.4 %convolution_convert_fusion = bf16[256,2048]{1,0:T(8,128)(2,1)} fusion(bf16[256,1024]{1,0:T(8,128)(2,1)S(1)} %gather_fusion.6, bf16[1024,2048]{1,0:T(8,128)(2,1)} %param.13), kind=kOutput, calls=%fused_computation.13 | convolution fusion | flops 1074266112 | bytes 5767168 | tf_op jit(solution)/shard_map/dot_general | solution.py:165
  331.7 63.4 %reduce-scatter.5.cloned.1.call-done = bf16[32,2048]{1,0:T(8,128)(2,1)} async-done(((bf16[256,2048]{1,0:T(8,128)(2,1)}), bf16[32,2048]{1,0:T(8,128)(2,1)}) %reduce-scatter.5.cloned.1.call-update) | async-done | bytes 131088 | tf_op jit(solution)/shard_map/reduce_scatter | solution.py:164
  (97 shorter events, 20.8 us)
Async XLA Ops:
  6.5 16.4 %copy-start = (s32[256,128]{1,0:T(8,128)S(1)}, s32[256,128]{1,0:T(8,128)}, u32[]{:S(2)}) copy-start(s32[256,128]{1,0:T(8,128)} %param.17) | copy-start | bytes 393220
  6.5 131.5 %all-reduce.3.cloned.1.call-start = ((), (), s32[]{:S(2)}) async-start(), calls=%async_computation.3 | async-start | bytes 5242880 | tf_op jit(solution)/shard_map/psum | solution.py:64
  21.0 0.7 copy-start.12
  21.0 1.1 copy-start.2
  21.0 2.5 copy-start.13
  21.0 117.0 %copy-start.8 = (f32[2560]{0:T(1024)S(1)}, f32[2560]{0:T(1024)}, u32[]{:S(2)}) copy-start(f32[2560]{0:T(1024)} %param.12) | copy-start | bytes 30724
  24.9 157.7 %copy-start.9 = (s32[32]{0:T(128)}, s32[32]{0:T(128)S(1)}, u32[]{:S(2)}) copy-start(s32[32]{0:T(128)S(1)} %get-tuple-element.6) | copy-start | bytes 388
  160.5 22.8 %all-to-all-start = ((bf16[4,64,2560]{2,1,0:T(8,128)(2,1)}), bf16[4,64,2560]{2,1,0:T(8,128)(2,1)S(1)}, u32[]{:S(2)}, u32[]{:S(2)}) async-start(bf16[4,64,2560]{2,1,0:T(8,128)(2,1)} %bitcast.8), calls=%async_computation | async-start | bytes 2621440 | tf_op jit(solution)/shard_map/all_to_all | solution.py:69
  164.1 153.6 %reduce-scatter.3.cloned.1.call-start = ((), (), s32[]{:S(2)}) async-start(), calls=%async_computation.4 | async-start | bytes 2359296 | tf_op jit(solution)/shard_map/reduce_scatter | solution.py:148
  164.3 20.6 %copy-start.11 = (s32[1024]{0:T(1024)}, s32[1024]{0:T(1024)S(1)}, u32[]{:S(2)}) copy-start(s32[1024]{0:T(1024)S(1)} %pad_clamp_fusion.2) | copy-start | bytes 12292
  182.6 2.0 copy-start.15
  183.4 4.4 %copy-start.5 = (pred[32,128]{1,0:T(8,128)(4,1)}, pred[32,128]{1,0:T(8,128)(4,1)S(1)}, u32[]{:S(2)}) copy-start(pred[32,128]{1,0:T(8,128)(4,1)S(1)} %fusion.25) | copy-start | bytes 12292
  202.1 3.5 copy-start.4
  203.5 37.2 %copy-start.6 = (pred[32,128]{1,0:T(8,128)(4,1)S(1)}, pred[32,128]{1,0:T(8,128)(4,1)}, u32[]{:S(2)}) copy-start(pred[32,128]{1,0:T(8,128)(4,1)} %copy-done.5) | copy-start | bytes 12292
  240.7 6.1 %copy-start.7 = (f32[32,64]{1,0:T(8,128)S(1)}, f32[32,64]{1,0:T(8,128)}, u32[]{:S(2)}) copy-start(f32[32,64]{1,0:T(8,128)} %exponential_select_fusion) | copy-start | bytes 24580
  240.7 6.4 %copy-start.10 = (s32[32]{0:T(128)S(1)}, s32[32]{0:T(128)}, u32[]{:S(2)}) copy-start(s32[32]{0:T(128)} %copy-done.9) | copy-start | bytes 388
  249.6 1.6 copy-start.16
  249.6 2.9 copy-start.14
  251.1 36.6 %copy-start.3 = (bf16[8,8,8,128]{3,1,2,0:T(8,128)(2,1)S(1)}, bf16[8,8,8,128]{3,1,2,0:T(8,128)(2,1)}, u32[]{:S(2)}) copy-start(bf16[8,8,8,128]{3,1,2,0:T(8,128)(2,1)} %get-tuple-element.13) | copy-start | bytes 393220
  251.1 143.9 %reduce-scatter.5.cloned.1.call-start = ((), (), s32[]{:S(2)}) async-start(), calls=%async_computation.5 | async-start | bytes 1179648 | tf_op jit(solution)/shard_map/reduce_scatter | solution.py:164
  326.1 69.0 %copy-start.1 = (s32[256,128]{1,0:T(8,128)S(1)}, s32[256,128]{1,0:T(8,128)}, u32[]{:S(2)}) copy-start(s32[256,128]{1,0:T(8,128)} %param.17) | copy-start | bytes 393220
Sparse Core Ops, SparseCore 0:
  21.2 116.7 all-reduce.2
  251.2 66.3 reduce-scatter.2
  331.8 63.1 reduce-scatter.4
where the time goes:
time: 403 us; the launch traced here: 402 us
  waiting for transfers between devices  206 us (51%)
  blocking collectives  85 us (21%)
  local copies, waits for them, and re-layouts  43.9 us (11%)
  matrix products  26.3 us (7%)
  other arithmetic  22.2 us (6%)
  between operations  14.2 us (4%)
    psum x1, waiting for transfers between devices, shards(): summed = lax.psum(partial_sum, 'seq')  113 us
    reduce_scatter x1, waiting for transfers between devices, shards(): lax.psum_scatter(jnp.dot(by_request, w_out, preferred_element_type=jnp.fl...  63.4 us
    pmax x1, blocking collectives, shards(): peak_score = lax.pmax(jnp.maximum(local_max, new_score), 'seq')  35 us
    unnamed x1, blocking collectives  33.8 us
    reduce_scatter x1, waiting for transfers between devices, shards(): lax.psum_scatter(scaled_out, 'seq', scatter_dimension=1, tiled=True)  29.7 us
    unnamed x45, local copies, waits for them, and re-layouts  22.6 us
    convert_element_type x1, other arithmetic, shards(): rotate_heads(summed + b_qkv[None, :], positions, col_start, HD, turned)  11.8 us
    all_gather x1, blocking collectives, shards(): lax.all_gather(hidden, 'grp', axis=0, tiled=True)  8.97 us
  transfers between devices with their start and end apart: 4, of which 3 were waited for; matrix products, arithmetic and copies ran while one was open for 6% of the time, Pallas kernels for 0%

commit v1 on v0

--- a/solution.py
+++ b/solution.py
@@ -61,7 +61,9 @@
     placed_at = restore[None, :] == request_ids[:, None]
     served_order = jnp.sum(jnp.where(placed_at, request_ids[None, :], 0), axis=1)
     served_ids = lax.dynamic_slice_in_dim(served_order, grp_index * group_size, group_size, 0)
-    summed = lax.psum(partial_sum, "seq")
+    summed = partial_sum
+    for hop in (1, 2, 4):
+        summed = summed + lax.ppermute(summed, "seq", [(dev, dev ^ hop) for dev in range(8)])
     fresh_rows = rotate_heads(summed + b_qkv[None, :], positions, col_start, HD, turned).astype(
         jnp.bfloat16
     )

time: 403 us -> 521 us (1.29)
  waiting for transfers between devices: 206 us -> 316 us
  starting transfers between devices: 3.81 us -> 9.68 us
    ppermute x0 -> x3, waiting for transfers between devices: none -> 223 us  [shards(): lax.ppermute(summed, 'seq', [(dev, dev ^ hop) for dev in range(8)])]
    psum x1 -> x0, waiting for transfers between devices: 113 us -> none  [shards(): summed = lax.psum(partial_sum, 'seq')]
    ppermute x0 -> x3, starting transfers between devices: none -> 5.88 us  [shards(): lax.ppermute(summed, 'seq', [(dev, dev ^ hop) for dev in range(8)])]
    unnamed x45 -> x49, local copies, waits for them, and re-layouts: 22.6 us -> 22 us
  transfers between devices with their start and end apart: 4 -> 6, of which waited for: 3 -> 5; matrix products, arithmetic and copies ran while one was open for 6% -> 5% of each run, Pallas kernels for 0% -> 0%
where the time goes in v1:
time: 521 us; the launch traced here: 520 us
  waiting for transfers between devices  316 us (61%)
  blocking collectives  87.3 us (17%)
  local copies, waits for them, and re-layouts  43.5 us (8%)
  matrix products  24.8 us (5%)
  other arithmetic  23.9 us (5%)
  between operations  14.6 us (3%)
  starting transfers between devices  9.68 us (2%)
    ppermute x3, waiting for transfers between devices, shards(): lax.ppermute(summed, 'seq', [(dev, dev ^ hop) for dev in range(8)])  223 us
    reduce_scatter x1, waiting for transfers between devices, shards(): lax.psum_scatter(jnp.dot(by_request, w_out, preferred_element_type=jnp.fl...  63.5 us
    pmax x1, blocking collectives, shards(): peak_score = lax.pmax(jnp.maximum(local_max, new_score), 'seq')  37.4 us
    unnamed x1, blocking collectives  33.8 us
    reduce_scatter x1, waiting for transfers between devices, shards(): lax.psum_scatter(scaled_out, 'seq', scatter_dimension=1, tiled=True)  29.6 us
    unnamed x49, local copies, waits for them, and re-layouts  22 us
    convert_element_type x1, other arithmetic, shards(): rotate_heads(summed + b_qkv[None, :], positions, col_start, HD, turned)  11.7 us
  transfers between devices with their start and end apart: 6, of which 5 were waited for; matrix products, arithmetic and copies ran while one was open for 5% of the time, Pallas kernels for 0%

profile of v1, /device:TPU:0, one launch (start us, length us, event | category | flops | bytes accessed | tf_op | source)
XLA Modules:
  0.0 519.9 jit_solution(12316151450606815911)
XLA Ops:
  6.5 9.0 %all_gather.6 = bf16[256,1024]{1,0:T(8,128)(2,1)S(1)} all-gather(bf16[64,1024]{1,0:T(8,128)(2,1)} %param.10), channel_id=1, replica_groups=mesh['seq'=8,'grp'=4] {'grp'}, dimensions={0}, use_global_device_ids=true | all-gather | bytes 655360 | tf_op jit(solution)/shard_map/all_gather | solution.py:54
  15.5 4.0 fusion.40
  21.1 57.6 %collective-permute-done = f32[256,2560]{1,0:T(8,128)S(1)} collective-permute-done((f32[256,2560]{1,0:T(8,128)S(1)}, f32[256,2560]{1,0:T(8,128)S(1)}, u32[]{:S(2)}, u32[]{:S(2)}) %collective-permute-start) | collective-permute-done | bytes 2621472 | tf_op jit(solution)/shard_map/ppermute | solution.py:66
  80.7 56.7 %collective-permute-done.1 = f32[256,2560]{1,0:T(8,128)S(1)} collective-permute-done((f32[256,2560]{1,0:T(8,128)S(1)}, f32[256,2560]{1,0:T(8,128)S(1)}, u32[]{:S(2)}, u32[]{:S(2)}) %collective-permute-start.1) | collective-permute-done | bytes 2621472 | tf_op jit(solution)/shard_map/ppermute | solution.py:66
  137.7 2.7 collective-permute-start.2
  143.6 108.8 %collective-permute-done.2 = f32[256,2560]{1,0:T(8,128)} collective-permute-done((f32[256,2560]{1,0:T(8,128)S(1)}, f32[256,2560]{1,0:T(8,128)}, u32[]{:S(2)}, u32[]{:S(2)}) %collective-permute-start.2) | collective-permute-done | bytes 2621472 | tf_op jit(solution)/shard_map/ppermute | solution.py:66
  252.4 2.9 add_add_fusion
  255.3 2.3 copy.46
  259.8 2.1 copy.47
  261.9 11.7 %select_convert_fusion = bf16[256,2560]{1,0:T(8,128)(2,1)S(1)} fusion(f32[256,2560]{1,0:T(8,128)} %copy-done.3, f32[256,2560]{1,0:T(8,128)} %copy.47, f32[2560]{0:T(1024)S(1)} %multiply_exponential_fusion, f32[256]{0:T(256)S(1)} %bitcast.120, f32[256]{0:T(256)S(1)} %bitcast.121, f32[256]{0:T(256)S(1)} %bitcast.119, ...), kind=kLoop, calls=%fused_computation.12 | loop fusion | flops 5242880 | bytes 6574592 | tf_op jit(solution)/shard_map/convert_element_type | solution.py:67
  273.6 2.5 gather_fusion.3
  276.1 3.5 all-to-all-start
  280.6 8.8 %copy.68 = bf16[512,8,8,128]{3,2,1,0:T(8,128)(2,1)} copy(bf16[512,8,8,128]{3,1,2,0:T(8,128)(2,1)} %bitcast.100) | data formatting | bytes 16777216
  289.4 8.8 %copy.69 = bf16[512,8,8,128]{3,2,1,0:T(8,128)(2,1)} copy(bf16[512,8,8,128]{3,1,2,0:T(8,128)(2,1)} %bitcast.101) | data formatting | bytes 16777216
  303.4 6.9 %select_reduce_fusion.1 = (f32[32,8,8]{2,1,0:T(8,128)S(1)}, f32[32,8,8,128]{3,2,1,0:T(8,128)S(1)}) fusion(pred[32,128]{1,0:T(8,128)(4,1)S(1)} %fusion.25, bf16[32,8,8,128]{3,2,1,0:T(8,128)(2,1)S(1)} %bitcast.109, bf16[32,128,8,128]{3,2,1,0:T(8,128)(2,1)} %bitcast.97), kind=kOutput, calls=%fused_computation.26 | convolution fusion | flops 67893248 | bytes 9973760 | tf_op jit(solution)/shard_map/pkgd,ptkd->pkgt/dot_general | solution.py:97
  313.5 2.0 gather_fusion.5
  321.3 37.4 %pmax.7 = f32[64,64]{0,1:T(8,128)S(1)} all-reduce(f32[64,64]{0,1:T(8,128)S(1)} %fusion.38), channel_id=1, replica_groups=mesh['seq'=8,'grp'=4] {'seq'}, use_global_device_ids=true, to_apply=%region_6.7 | all-reduce | flops 4096 | bytes 32768 | tf_op jit(solution)/shard_map/pmax | solution.py:144
  358.7 6.1 %fusion = f32[32,8,8,128]{3,2,1,0:T(8,128)S(1)} fusion(bf16[32,128,8,128]{3,2,1,0:T(8,128)(2,1)} %bitcast.96, f32[32,8,8,128]{3,2,1,0:T(8,128)S(1)} %get-tuple-element.21, f32[32,8,8]{2,1,0:T(8,128)S(1)} %get-tuple-element.20, pred[32,128]{1,0:T(8,128)(4,1)S(1)} %copy-done.8), kind=kOutput, calls=%fused_computation.7 | convolution fusion | flops 67895296 | bytes 10498048 | tf_op jit(solution)/shard_map/pkgt,ptkd->pkgd/dot_general | solution.py:106
  365.1 2.5 multiply_bitcast_fusion
  371.7 33.8 %all-reduce = f32[64,64]{0,1:T(8,128)S(1)} all-reduce(f32[64,64]{0,1:T(8,128)S(1)} %convolution_multiply_fusion), channel_id=3, replica_groups=mesh['seq'=8,'grp'=4] {'seq'}, use_global_device_ids=true, to_apply=%region_9.10.clone | all-reduce | flops 4096 | bytes 32768
  405.9 29.6 %reduce-scatter.3.cloned.1.call-done = f32[64,1024]{1,0:T(8,128)} async-done(((f32[64,8192]{1,0:T(8,128)}), f32[64,1024]{1,0:T(8,128)}) %reduce-scatter.3.cloned.1.call-update) | async-done | bytes 262160 | tf_op jit(solution)/shard_map/reduce_scatter | solution.py:150
  436.8 7.2 %all_gather.7 = bf16[256,1024]{1,0:T(8,128)(2,1)S(1)} all-gather(bf16[64,1024]{1,0:T(8,128)(2,1)S(1)} %bitcast.113), channel_id=1, replica_groups=mesh['seq'=8,'grp'=4] {'grp'}, dimensions={0}, use_global_device_ids=true | all-gather | bytes 655360 | tf_op jit(solution)/shard_map/all_gather | solution.py:164
  445.1 4.4 convolution_convert_fusion
  449.6 63.5 %reduce-scatter.5.cloned.1.call-done = bf16[32,2048]{1,0:T(8,128)(2,1)} async-done(((bf16[256,2048]{1,0:T(8,128)(2,1)}), bf16[32,2048]{1,0:T(8,128)(2,1)}) %reduce-scatter.5.cloned.1.call-update) | async-done | bytes 131088 | tf_op jit(solution)/shard_map/reduce_scatter | solution.py:166
  (106 shorter events, 30.7 us)
Async XLA Ops:
  6.5 135.0 %copy-start = (s32[256,128]{1,0:T(8,128)S(1)}, s32[256,128]{1,0:T(8,128)}, u32[]{:S(2)}) copy-start(s32[256,128]{1,0:T(8,128)} %param.17) | copy-start | bytes 393220
  19.5 59.2 %collective-permute-start = (f32[256,2560]{1,0:T(8,128)S(1)}, f32[256,2560]{1,0:T(8,128)S(1)}, u32[]{:S(2)}, u32[]{:S(2)}) collective-permute-start(f32[256,2560]{1,0:T(8,128)S(1)} %fusion.40), channel_id=1, source_target_pairs={{0,4},{4,0},{8,12},{12,8},{16,20},{20,16},{24,28},{28,24},{1,5},{5... | collective-permute-start | bytes 7864328 | tf_op jit(solution)/shard_map/ppermute | solution.py:66
  79.0 61.4 %copy-start.14 = (s32[256]{0:T(256)S(1)}, s32[256]{0:T(256)}, u32[]{:S(2)}) copy-start(s32[256]{0:T(256)} %param.19) | copy-start | bytes 3076
  79.0 61.7 %copy-start.2 = (s32[256]{0:T(256)S(1)}, s32[256]{0:T(256)}, u32[]{:S(2)}) copy-start(s32[256]{0:T(256)} %param.16) | copy-start | bytes 3076
  79.0 63.1 %copy-start.15 = (s32[3,256]{1,0:T(4,128)S(1)}, s32[3,256]{1,0:T(4,128)}, u32[]{:S(2)}) copy-start(s32[3,256]{1,0:T(4,128)} %param.18) | copy-start | bytes 9220
  79.0 173.3 %copy-start.10 = (f32[2560]{0:T(1024)S(1)}, f32[2560]{0:T(1024)}, u32[]{:S(2)}) copy-start(f32[2560]{0:T(1024)} %param.12) | copy-start | bytes 30724
  79.1 58.3 %collective-permute-start.1 = (f32[256,2560]{1,0:T(8,128)S(1)}, f32[256,2560]{1,0:T(8,128)S(1)}, u32[]{:S(2)}, u32[]{:S(2)}) collective-permute-start(f32[256,2560]{1,0:T(8,128)S(1)} %add.155), channel_id=1, source_target_pairs={{0,8},{4,12},{8,0},{12,4},{16,24},{20,28},{24,16},{28,20},{1,9},{5... | collective-permute-start | bytes 7864328 | tf_op jit(solution)/shard_map/ppermute | solution.py:66
  137.7 5.9 %copy-start.4 = (f32[256,2560]{1,0:T(8,128)}, f32[256,2560]{1,0:T(8,128)S(1)}, u32[]{:S(2)}) copy-start(f32[256,2560]{1,0:T(8,128)S(1)} %add.156) | copy-start | bytes 7864324
  137.7 114.7 %collective-permute-start.2 = (f32[256,2560]{1,0:T(8,128)S(1)}, f32[256,2560]{1,0:T(8,128)}, u32[]{:S(2)}, u32[]{:S(2)}) collective-permute-start(f32[256,2560]{1,0:T(8,128)S(1)} %add.156), channel_id=1, source_target_pairs={{0,16},{4,20},{8,24},{12,28},{16,0},{20,4},{24,8},{28,12},{1,17},{... | collective-permute-start | bytes 7864328 | tf_op jit(solution)/shard_map/ppermute | solution.py:66
  143.5 154.6 %copy-start.11 = (s32[32]{0:T(128)}, s32[32]{0:T(128)S(1)}, u32[]{:S(2)}) copy-start(s32[32]{0:T(128)S(1)} %get-tuple-element.6) | copy-start | bytes 388
  255.3 2.3 copy-start.3
  276.1 22.9 %all-to-all-start = ((bf16[4,64,2560]{2,1,0:T(8,128)(2,1)}), bf16[4,64,2560]{2,1,0:T(8,128)(2,1)S(1)}, u32[]{:S(2)}, u32[]{:S(2)}) async-start(bf16[4,64,2560]{2,1,0:T(8,128)(2,1)} %bitcast.8), calls=%async_computation | async-start | bytes 2621440 | tf_op jit(solution)/shard_map/all_to_all | solution.py:71
  279.6 155.9 %reduce-scatter.3.cloned.1.call-start = ((), (), s32[]{:S(2)}) async-start(), calls=%async_computation.3 | async-start | bytes 2359296 | tf_op jit(solution)/shard_map/reduce_scatter | solution.py:150
  279.9 20.6 %copy-start.13 = (s32[1024]{0:T(1024)}, s32[1024]{0:T(1024)S(1)}, u32[]{:S(2)}) copy-start(s32[1024]{0:T(1024)S(1)} %pad_clamp_fusion.2) | copy-start | bytes 12292
  298.2 2.0 copy-start.17
  298.9 4.4 copy-start.7
  317.7 3.5 copy-start.6
  319.1 39.5 %copy-start.8 = (pred[32,128]{1,0:T(8,128)(4,1)S(1)}, pred[32,128]{1,0:T(8,128)(4,1)}, u32[]{:S(2)}) copy-start(pred[32,128]{1,0:T(8,128)(4,1)} %copy-done.7) | copy-start | bytes 12292
  358.7 6.1 %copy-start.9 = (f32[32,64]{1,0:T(8,128)S(1)}, f32[32,64]{1,0:T(8,128)}, u32[]{:S(2)}) copy-start(f32[32,64]{1,0:T(8,128)} %exponential_select_fusion) | copy-start | bytes 24580
  358.7 6.4 %copy-start.12 = (s32[32]{0:T(128)S(1)}, s32[32]{0:T(128)}, u32[]{:S(2)}) copy-start(s32[32]{0:T(128)} %copy-done.11) | copy-start | bytes 388
  367.6 2.9 copy-start.16
  369.1 36.5 %copy-start.5 = (bf16[8,8,8,128]{3,1,2,0:T(8,128)(2,1)S(1)}, bf16[8,8,8,128]{3,1,2,0:T(8,128)(2,1)}, u32[]{:S(2)}) copy-start(bf16[8,8,8,128]{3,1,2,0:T(8,128)(2,1)} %get-tuple-element.13) | copy-start | bytes 393220
  369.1 143.9 %reduce-scatter.5.cloned.1.call-start = ((), (), s32[]{:S(2)}) async-start(), calls=%async_computation.4 | async-start | bytes 1179648 | tf_op jit(solution)/shard_map/reduce_scatter | solution.py:166
  443.9 69.1 %copy-start.1 = (s32[256,128]{1,0:T(8,128)S(1)}, s32[256,128]{1,0:T(8,128)}, u32[]{:S(2)}) copy-start(s32[256,128]{1,0:T(8,128)} %param.17) | copy-start | bytes 393220
  (1 other events, 1.6 us)
Sparse Core Ops, SparseCore 0:
  369.2 66.2 reduce-scatter.2
  449.7 63.2 reduce-scatter.4
